TPU v7x, 32 devices: a whole 2x2x4 slice. The times are simulated.
32 devices in a mesh: owner: 4 (over y, core), rows: 8 (over z, x).
Axes of the slice: x: 2, y: 2, z: 4, core: 2. Of those that a mesh axis runs over, the one named last changes fastest.
Arguments:
- train_gate: float32 [64, 2048, 1024], P('owner', 'rows'), may hold values from -0.1875 to 0.1875
- other_gate: bfloat16 [64, 2048, 1024], P('owner', 'rows'), may hold values from -0.0625 to 0.0625
- train_up: float32 [64, 2048, 1024], P('owner', 'rows'), may hold values from -0.1875 to 0.1875
- other_up: bfloat16 [64, 2048, 1024], P('owner', 'rows'), may hold values from -0.0625 to 0.0625
- train_down: float32 [64, 1024, 2048], P('owner', None, 'rows'), may hold values from -0.25 to 0.25
- other_down: bfloat16 [64, 1024, 2048], P('owner', None, 'rows'), may hold values from -0.09375 to 0.09375
- router_weight: float32 [2048, 64], P('rows', 'owner'), may hold values from -0.125 to 0.125
- router_gain: float32 [2048], P('rows'), may hold values from 0.25 to 1.75
Outputs:
- ready_gate: bfloat16 [64, 2048, 1024], P('owner', None, 'rows')
- ready_up: bfloat16 [64, 2048, 1024], P('owner', None, 'rows')
- ready_down: bfloat16 [64, 1024, 2048], P('owner', 'rows')
- scale_gate: float32 [64, 1024], P('owner', 'rows')
- scale_up: float32 [64, 1024], P('owner', 'rows')
- scale_down: float32 [64, 1024], P('owner', 'rows')
- serve_router: bfloat16 [2048, 64], replicated
All inputs are finite; a program needn't handle non-finite values. Where the computation divides by a largest or mean magnitude, that divisor is 1e-20 or more.
Results may differ from a plain program's by a relative error of at most 0.001.
Values may be sent and summed in bfloat16 or wider, within the bound.
A program may use at most 192 MiB of HBM per device.

v0:
```python
import jax
import jax.numpy as jnp
from jax import lax
from jax.sharding import PartitionSpec as P


def shards(
    train_gate, other_gate, train_up, other_up, train_down, other_down, router_weight, router_gain
):
    latest_gate = train_gate + other_gate.astype(jnp.float32)
    latest_up = train_up + other_up.astype(jnp.float32)
    latest_down = train_down + other_down.astype(jnp.float32)
    scale_gate, scale_up, scale_down = lax.pmax(
        (
            jnp.max(jnp.abs(latest_gate), axis=1),
            jnp.max(jnp.abs(latest_up), axis=1),
            jnp.max(jnp.abs(latest_down), axis=2),
        ),
        "rows",
    )
    narrow_gate, narrow_up, narrow_down = (
        (latest_gate / jnp.expand_dims(scale_gate, 1)).astype(jnp.bfloat16),
        (latest_up / jnp.expand_dims(scale_up, 1)).astype(jnp.bfloat16),
        (latest_down / jnp.expand_dims(scale_down, 2)).astype(jnp.bfloat16),
    )
    ready_gate, ready_up = (
        lax.all_to_all(narrow_gate, "rows", split_axis=2, concat_axis=1, tiled=True),
        lax.all_to_all(narrow_up, "rows", split_axis=2, concat_axis=1, tiled=True),
    )
    ready_down = lax.all_to_all(narrow_down, "rows", split_axis=1, concat_axis=2, tiled=True)
    scale_gate = lax.dynamic_slice_in_dim(
        scale_gate, lax.axis_index("rows") * ready_gate.shape[2], ready_gate.shape[2], axis=1
    )
    scale_up = lax.dynamic_slice_in_dim(
        scale_up, lax.axis_index("rows") * ready_up.shape[2], ready_up.shape[2], axis=1
    )
    scale_down = lax.dynamic_slice_in_dim(
        scale_down, lax.axis_index("rows") * ready_down.shape[1], ready_down.shape[1], axis=1
    )
    part_router = (router_weight * router_gain[:, None]).astype(jnp.bfloat16)
    row_router = lax.all_gather(part_router, "rows", axis=0, tiled=True)
    serve_router = lax.all_gather(row_router, "owner", axis=1, tiled=True)
    return (ready_gate, ready_up, ready_down, scale_gate, scale_up, scale_down, serve_router)


def solution(mesh):
    placed = (
        P("owner", "rows", None),
        P("owner", "rows", None),
        P("owner", "rows", None),
        P("owner", "rows", None),
        P("owner", None, "rows"),
        P("owner", None, "rows"),
        P("rows", "owner"),
        P("rows"),
    )
    return jax.shard_map(
        shards,
        mesh=mesh,
        in_specs=placed,
        out_specs=(
            P("owner", None, "rows"),
            P("owner", None, "rows"),
            P("owner", "rows", None),
            P("owner", "rows"),
            P("owner", "rows"),
            P("owner", "rows"),
            P(),
        ),
        check_vma=False,
    )
```

profile of v0, /device:TPU:0, one launch (start us, length us, event | category | flops | bytes accessed | tf_op | source)
XLA Modules:
  0.0 877.2 jit_solution(6322543164802641597)
XLA Ops:
  7.2 0.0 all-reduce.3.cloned.1.call-start
  7.2 17.6 %copy.34 = f32[16,256,1024]{1,0,2:T(8,128)} copy(f32[16,256,1024]{2,1,0:T(8,128)} %param.10) | data formatting | bytes 33554432 | tf_op args[2]
  24.8 12.5 %copy.33 = bf16[16,256,1024]{1,0,2:T(8,128)(2,1)} copy(bf16[16,256,1024]{2,1,0:T(8,128)(2,1)} %param.11) | data formatting | bytes 16777216 | tf_op args[3]
  37.3 17.6 %copy.31 = f32[16,256,1024]{1,0,2:T(8,128)} copy(f32[16,256,1024]{2,1,0:T(8,128)} %param.8) | data formatting | bytes 33554432 | tf_op args[0]
  54.9 12.5 %copy.30 = bf16[16,256,1024]{1,0,2:T(8,128)(2,1)} copy(bf16[16,256,1024]{2,1,0:T(8,128)(2,1)} %param.9) | data formatting | bytes 16777216 | tf_op args[1]
  67.4 11.1 %abs_reduce_fusion.1 = f32[16,1024]{0,1:T(8,128)} fusion(f32[16,256,1024]{1,0,2:T(8,128)} %copy.34, bf16[16,256,1024]{1,0,2:T(8,128)(2,1)} %copy.33), kind=kLoop, calls=%fused_computation.4 | loop fusion | flops 16760832 | bytes 25231360 | tf_op jit(solution)/shard_map/reduce_max | solution.py:16
  78.5 2.1 copy-done
  80.6 2.4 copy-done.1
  83.0 4.3 abs_reduce_fusion.2
  87.3 0.0 slice-done
  87.3 29.3 %abs_reduce_fusion = f32[16,1024]{0,1:T(8,128)} fusion(f32[16,1024,256]{2,1,0:T(8,128)} %param.12, bf16[16,1024,256]{2,1,0:T(8,128)(2,1)S(1)} %bitcast.14), kind=kLoop, calls=%fused_computation.2 | loop fusion | flops 16760832 | bytes 25231360 | tf_op jit(solution)/shard_map/reduce_max | solution.py:17
  116.5 0.0 all-reduce.3.cloned.1.call-update
  116.6 92.5 %all-reduce.3.cloned.1.call-done = (f32[16,1024]{0,1:T(8,128)}, f32[16,1024]{0,1:T(8,128)}, f32[16,1024]{0,1:T(8,128)}) async-done(((f32[16,1024]{0,1:T(8,128)}, f32[16,1024]{0,1:T(8,128)}, f32[16,1024]{0,1:T(8,128)}), (f32[16,1024]{0,1:T(8,128)}, f32[16,1024]{0,1:T(8,128)}, f32[16,1024]{0,1:T(8,128)})) %all-reduce.3.cloned.1.call-update) | async-done | bytes 196624 | tf_op jit(solution)/shard_map/pmax | solution.py:13
  209.0 20.5 %divide_convert_fusion.1 = (bf16[16,256,1024]{1,0,2:T(8,128)(2,1)}, bf16[16,256,1024]{1,0,2:T(8,128)(2,1)S(1)}) fusion(f32[16,256,1024]{1,0,2:T(8,128)} %copy.34, bf16[16,256,1024]{1,0,2:T(8,128)(2,1)} %copy.33, f32[16,1024]{0,1:T(8,128)} %get-tuple-element.15, f32[16,1024]{0,1:T(8,128)} %get-tuple-element.14, f32[16,256,1024]{1,0,2:T(8,128)} %copy.31, ...), kind=kLoop, calls=%fused_computation.3 | loop fusion | flops 33554432 | bytes 67239936 | tf_op jit(solution)/shard_map/convert_element_type | solution.py:23
  229.6 187.0 %all_to_all.54 = bf16[16,256,1024]{1,0,2:T(8,128)(2,1)} all-to-all(bf16[16,256,1024]{1,0,2:T(8,128)(2,1)S(1)} %get-tuple-element.18), channel_id=1, replica_groups=mesh['owner'=4,'rows'=8] {'rows'}, dimensions={2} | all-to-all | bytes 16777216 | tf_op jit(solution)/shard_map/all_to_all | solution.py:27
  416.6 4.9 all-to-all-start.1
  421.5 23.8 %divide_convert_fusion = bf16[16,1024,256]{2,0,1:T(8,128)(2,1)} fusion(f32[16,1024,256]{2,1,0:T(8,128)} %param.12, f32[16,1024]{0,1:T(8,128)S(1)} %copy-done.2, bf16[16,1024,256]{2,1,0:T(8,128)(2,1)} %param.13), kind=kLoop, calls=%fused_computation.1 | loop fusion | flops 16777216 | bytes 33619968 | tf_op jit(solution)/shard_map/convert_element_type | solution.py:24
  445.3 158.3 %all-to-all-done.1 = bf16[16,256,1024]{1,0,2:T(8,128)(2,1)} async-done(((bf16[16,256,1024]{1,0,2:T(8,128)(2,1)}), bf16[16,256,1024]{1,0,2:T(8,128)(2,1)}, u32[]{:S(2)}, u32[]{:S(2)}) %all-to-all-start.1) | async-done | bytes 8388640 | tf_op jit(solution)/shard_map/all_to_all | solution.py:28
  603.6 5.0 all-to-all-start.2
  608.7 201.9 %all_gather.6 = bf16[2048,16]{0,1:T(8,128)(2,1)S(1)} all-gather(bf16[256,16]{0,1:T(8,128)(2,1)S(1)} %multiply_convert_fusion), channel_id=1, replica_groups=mesh['owner'=4,'rows'=8] {'rows'}, dimensions={0}, use_global_device_ids=true | all-gather | bytes 73728 | tf_op jit(solution)/shard_map/all_gather | solution.py:41
  810.6 6.0 all_gather.7
  816.5 0.8 constant_dynamic-slice_fusion
  817.4 0.7 copy.40
  818.1 0.7 copy.41
  818.7 0.8 constant_dynamic-slice_fusion.2
  819.6 0.7 copy.39
  820.2 12.3 %copy.32 = bf16[16,8,256,128]{3,2,1,0:T(8,128)(2,1)} copy(bf16[16,8,256,128]{2,0,3,1:T(8,128)(2,1)} %bitcast.15) | data formatting | bytes 16777216 | tf_op jit(solution)/shard_map/all_to_all | solution.py:27
  832.5 12.3 %copy.35 = bf16[16,8,256,128]{3,2,1,0:T(8,128)(2,1)} copy(bf16[16,8,256,128]{2,0,3,1:T(8,128)(2,1)} %bitcast.4) | data formatting | bytes 16777216 | tf_op jit(solution)/shard_map/all_to_all | solution.py:28
  844.8 0.0 all-to-all-done.2
  844.8 11.4 %copy.38 = bf16[16,128,8,256]{3,2,1,0:T(8,128)(2,1)} copy(bf16[16,128,8,256]{3,0,1,2:T(8,128)(2,1)} %bitcast.7) | data formatting | bytes 16777216 | tf_op jit(solution)/shard_map/all_to_all | solution.py:30
  856.2 13.4 %all_to_all.50 = bf16[16,128,2048]{2,1,0:T(8,128)(2,1)} reshape(bf16[16,128,8,256]{3,2,1,0:T(8,128)(2,1)} %copy.38) | data formatting | bytes 16777216 | tf_op jit(solution)/shard_map/all_to_all | solution.py:30
  869.6 0.7 copy.53
  (13 shorter events, 0.0 us)
Async XLA Ops:
  7.2 201.9 %all-reduce.3.cloned.1.call-start = ((), (), s32[]{:S(2)}) async-start(), calls=%async_computation.3 | async-start | bytes 3145728 | tf_op jit(solution)/shard_map/pmax | solution.py:13
  67.4 13.2 %copy-start = (f32[16,256,1024]{1,0,2:T(8,128)S(1)}, f32[16,256,1024]{1,0,2:T(8,128)}, u32[]{:S(2)}) copy-start(f32[16,256,1024]{1,0,2:T(8,128)} %copy.31) | copy-start | bytes 50331652
  67.4 15.6 %copy-start.1 = (bf16[16,256,1024]{1,0,2:T(8,128)(2,1)S(1)}, bf16[16,256,1024]{1,0,2:T(8,128)(2,1)}, u32[]{:S(2)}) copy-start(bf16[16,256,1024]{1,0,2:T(8,128)(2,1)} %copy.30) | copy-start | bytes 25165828
  67.4 19.9 %slice-start = ((s8[8388608]{0:T(1024)(128)(4,1)}), s8[4194304]{0:T(1024)(128)(4,1)S(1)}, s32[]{:S(2)}) async-start(s8[8388608]{0:T(1024)(128)(4,1)} %bitcast.13), calls=%async_computation.4 | async-start | bytes 8388608
  83.0 4.3 slice-start.1
  229.6 192.0 %copy-start.2 = (f32[16,1024]{0,1:T(8,128)S(1)}, f32[16,1024]{0,1:T(8,128)}, u32[]{:S(2)}) copy-start(f32[16,1024]{0,1:T(8,128)} %get-tuple-element.16) | copy-start | bytes 196612
  416.6 187.0 %all-to-all-start.1 = ((bf16[16,256,1024]{1,0,2:T(8,128)(2,1)}), bf16[16,256,1024]{1,0,2:T(8,128)(2,1)}, u32[]{:S(2)}, u32[]{:S(2)}) async-start(bf16[16,256,1024]{1,0,2:T(8,128)(2,1)} %get-tuple-element.17), calls=%async_computation.1 | async-start | bytes 16777216 | tf_op jit(solution)/shard_map/all_to_all | solution.py:28
  445.3 163.3 %copy-start.3 = (f32[256,16]{0,1:T(8,128)S(1)}, f32[256,16]{0,1:T(8,128)}, u32[]{:S(2)}) copy-start(f32[256,16]{0,1:T(8,128)} %param.14) | copy-start | bytes 49156
  445.3 163.3 %copy-start.4 = (f32[256]{0:T(256)S(1)}, f32[256]{0:T(256)}, u32[]{:S(2)}) copy-start(f32[256]{0:T(256)} %param.15) | copy-start | bytes 3076
  603.6 241.2 %all-to-all-start.2 = ((bf16[16,1024,256]{2,0,1:T(8,128)(2,1)}), bf16[16,1024,256]{2,0,1:T(8,128)(2,1)}, u32[]{:S(2)}, u32[]{:S(2)}) async-start(bf16[16,1024,256]{2,0,1:T(8,128)(2,1)} %divide_convert_fusion), calls=%async_computation.2 | async-start | bytes 16777216 | tf_op jit(solution)/shard_map/all_to_all | solution.py:30
Sparse Core Ops, SparseCore 0:
  116.7 92.2 all-reduce.2
where the time goes:
time: 880 us; the launch traced here: 877 us
  blocking collectives  395 us (45%)
  waiting for transfers between devices  251 us (29%)
  local copies, waits for them, and re-layouts  118 us (13%)
  other arithmetic  88.9 us (10%)
  between operations  14.1 us (2%)
  starting transfers between devices  10 us (1%)
    all_gather x1, blocking collectives, shards(): row_router = lax.all_gather(part_router, 'rows', axis=0, tiled=True)  202 us
    all_to_all x1, blocking collectives, shards(): lax.all_to_all(narrow_gate, 'rows', split_axis=2, concat_axis=1, tiled=True)  187 us
    all_to_all x1, waiting for transfers between devices, shards(): lax.all_to_all(narrow_up, 'rows', split_axis=2, concat_axis=1, tiled=True)  158 us
    pmax x1, waiting for transfers between devices, shards(): lax.pmax((jnp.max(jnp.abs(latest_gate), axis=1), jnp.max(jnp.abs(latest_u...  92.5 us
    unnamed x22, local copies, waits for them, and re-layouts  67.4 us
    reduce_max x1, other arithmetic, shards(): jnp.max(jnp.abs(latest_down), axis=2)  29.3 us
    all_to_all x2, local copies, waits for them, and re-layouts, shards(): lax.all_to_all(narrow_down, 'rows', split_axis=1, concat_axis=2, tiled=True)  24.8 us
    convert_element_type x1, other arithmetic, shards(): (latest_down / jnp.expand_dims(scale_down, 2)).astype(jnp.bfloat16)  23.8 us
  transfers between devices with their start and end apart: 3, of which 2 were waited for; matrix products, arithmetic and copies ran while one was open for 6% of the time, Pallas kernels for 0%

commit v1 on v0

--- a/solution.py
+++ b/solution.py
@@ -2,6 +2,16 @@
 import jax.numpy as jnp
 from jax import lax
 from jax.sharding import PartitionSpec as P
+
+tails_launch = lambda frame, mesh_dim, out_dim, dim_k: jnp.concatenate(
+    jax.lax.all_to_all(
+        jnp.stack(jnp.split(frame, jax.lax.axis_size(mesh_dim), axis=out_dim)),
+        axis_name=mesh_dim,
+        concat_axis=0,
+        split_axis=0,
+    ),
+    axis=dim_k,
+)
 
 
 def shards(
@@ -24,7 +34,7 @@
         (latest_down / jnp.expand_dims(scale_down, 2)).astype(jnp.bfloat16),
     )
     ready_gate, ready_up = (
-        lax.all_to_all(narrow_gate, "rows", split_axis=2, concat_axis=1, tiled=True),
+        tails_launch(narrow_gate, "rows", 2, 1),
         lax.all_to_all(narrow_up, "rows", split_axis=2, concat_axis=1, tiled=True),
     )
     ready_down = lax.all_to_all(narrow_down, "rows", split_axis=1, concat_axis=2, tiled=True)

time: 880 us -> 822 us (0.934)
  blocking collectives: 395 us -> 208 us
  waiting for transfers between devices: 251 us -> 404 us
  local copies, waits for them, and re-layouts: 118 us -> 88.9 us
    all_to_all x1 -> x0, blocking collectives: 187 us -> none  [shards(): lax.all_to_all(narrow_gate, 'rows', split_axis=2, concat_axis=1, tiled=True)]
    all_to_all x1, waiting for transfers between devices: 0.01 us -> 163 us  [shards(): lax.all_to_all(narrow_down, 'rows', split_axis=1, concat_axis=2, tiled=True)]
    unnamed x22 -> x34, local copies, waits for them, and re-layouts: 67.4 us -> 41.2 us
    all_to_all x1 -> x0, local copies, waits for them, and re-layouts: 12.3 us -> none  [shards(): lax.all_to_all(narrow_gate, 'rows', split_axis=2, concat_axis=1, tiled=True)]
    pmax x1, waiting for transfers between devices: 92.5 us -> 82.4 us  [shards(): lax.pmax((jnp.max(jnp.abs(latest_gate), axis=1), jnp.max(jnp.abs(latest_u...]
    convert_element_type x0 -> x1, other arithmetic: none -> 9.39 us  [shards(): (latest_gate / jnp.expand_dims(scale_gate, 1)).astype(jnp.bfloat16)]
  transfers between devices with their start and end apart: 3 -> 4, of which waited for: 2 -> 3; matrix products, arithmetic and copies ran while one was open for 6% -> 8% of each run, Pallas kernels for 0% -> 0%
where the time goes in v1:
time: 822 us; the launch traced here: 820 us
  waiting for transfers between devices  404 us (49%)
  blocking collectives  208 us (25%)
  other arithmetic  89.9 us (11%)
  local copies, waits for them, and re-layouts  88.9 us (11%)
  starting transfers between devices  15.2 us (2%)
  between operations  14.2 us (2%)
    all_gather x1, blocking collectives, shards(): row_router = lax.all_gather(part_router, 'rows', axis=0, tiled=True)  202 us
    all_to_all x1, waiting for transfers between devices, shards(): lax.all_to_all(narrow_down, 'rows', split_axis=1, concat_axis=2, tiled=True)  163 us
    all_to_all x1, waiting for transfers between devices, shards(): lax.all_to_all(narrow_up, 'rows', split_axis=2, concat_axis=1, tiled=True)  159 us
    pmax x1, waiting for transfers between devices, shards(): lax.pmax((jnp.max(jnp.abs(latest_gate), axis=1), jnp.max(jnp.abs(latest_u...  82.4 us
    unnamed x34, local copies, waits for them, and re-layouts  41.2 us
    reduce_max x1, other arithmetic, shards(): jnp.max(jnp.abs(latest_down), axis=2)  30.1 us
    all_to_all x2, local copies, waits for them, and re-layouts, shards(): lax.all_to_all(narrow_down, 'rows', split_axis=1, concat_axis=2, tiled=True)  24.8 us
    convert_element_type x1, other arithmetic, shards(): (latest_down / jnp.expand_dims(scale_down, 2)).astype(jnp.bfloat16)  23.8 us
  transfers between devices with their start and end apart: 4, of which 3 were waited for; matrix products, arithmetic and copies ran while one was open for 8% of the time, Pallas kernels for 0%

profile of v1, /device:TPU:0, one launch (start us, length us, event | category | flops | bytes accessed | tf_op | source)
XLA Modules:
  0.0 820.1 jit_solution(4641286640537155644)
XLA Ops:
  7.2 12.5 %copy.28 = bf16[16,256,1024]{1,0,2:T(8,128)(2,1)} copy(bf16[16,256,1024]{2,1,0:T(8,128)(2,1)} %param.11) | data formatting | bytes 16777216 | tf_op args[3]
  19.7 17.6 %copy.29 = f32[16,256,1024]{1,0,2:T(8,128)} copy(f32[16,256,1024]{2,1,0:T(8,128)} %param.10) | data formatting | bytes 33554432 | tf_op args[2]
  37.3 10.3 %abs_reduce_fusion.2 = f32[16,1024]{1,0:T(8,128)} fusion(f32[16,256,1024]{2,1,0:T(8,128)} %param.8, bf16[16,256,1024]{2,1,0:T(8,128)(2,1)} %param.9), kind=kLoop, calls=%fused_computation.7 | loop fusion | flops 16760832 | bytes 25231360 | tf_op jit(solution)/shard_map/reduce_max | solution.py:25
  47.9 30.1 %abs_reduce_fusion = f32[16,1024]{0,1:T(8,128)} fusion(f32[16,1024,256]{2,1,0:T(8,128)} %param.12, bf16[16,1024,256]{2,1,0:T(8,128)(2,1)S(1)} %copy-done), kind=kLoop, calls=%fused_computation.2 | loop fusion | flops 16760832 | bytes 25231360 | tf_op jit(solution)/shard_map/reduce_max | solution.py:27
  78.1 4.3 abs_reduce_fusion.1
  82.4 82.4 %all-reduce.3.cloned.1.call-done = (f32[16,1024]{1,0:T(8,128)}, f32[16,1024]{0,1:T(8,128)}, f32[16,1024]{0,1:T(8,128)}) async-done(((f32[16,1024]{1,0:T(8,128)}, f32[16,1024]{0,1:T(8,128)}, f32[16,1024]{0,1:T(8,128)}), (f32[16,1024]{1,0:T(8,128)}, f32[16,1024]{0,1:T(8,128)}, f32[16,1024]{0,1:T(8,128)})) %all-reduce.3.cloned.1.call-update) | async-done | bytes 196624 | tf_op jit(solution)/shard_map/pmax | solution.py:23
  164.8 12.1 %divide_convert_fusion.1 = bf16[16,256,1024]{1,0,2:T(8,128)(2,1)} fusion(f32[16,256,1024]{1,0,2:T(8,128)} %copy.29, bf16[16,256,1024]{1,0,2:T(8,128)(2,1)} %copy.28, f32[16,1024]{0,1:T(8,128)} %get-tuple-element.15), kind=kLoop, calls=%fused_computation.3 | loop fusion | flops 16777216 | bytes 33619968 | tf_op jit(solution)/shard_map/convert_element_type | solution.py:33
  176.9 5.3 all-to-all-start.1
  182.1 23.8 %divide_convert_fusion = bf16[16,1024,256]{2,0,1:T(8,128)(2,1)} fusion(f32[16,1024,256]{2,1,0:T(8,128)} %param.12, f32[16,1024]{0,1:T(8,128)S(1)} %copy-done.1, bf16[16,1024,256]{2,1,0:T(8,128)(2,1)} %param.13), kind=kLoop, calls=%fused_computation.1 | loop fusion | flops 16777216 | bytes 33619968 | tf_op jit(solution)/shard_map/convert_element_type | solution.py:34
  205.9 158.7 %all-to-all-done.1 = bf16[16,256,1024]{1,0,2:T(8,128)(2,1)} async-done(((bf16[16,256,1024]{1,0,2:T(8,128)(2,1)}), bf16[16,256,1024]{1,0,2:T(8,128)(2,1)}, u32[]{:S(2)}, u32[]{:S(2)}) %all-to-all-start.1) | async-done | bytes 8388640 | tf_op jit(solution)/shard_map/all_to_all | solution.py:38
  364.7 5.0 all-to-all-start.2
  369.7 9.4 %divide_convert_fusion.2 = bf16[16,256,1024]{2,1,0:T(8,128)(2,1)S(1)} fusion(f32[16,256,1024]{2,1,0:T(8,128)} %param.8, bf16[16,256,1024]{2,1,0:T(8,128)(2,1)} %param.9, f32[16,1024]{1,0:T(8,128)S(1)} %copy-done.2), kind=kLoop, calls=%fused_computation.6 | loop fusion | flops 16777216 | bytes 33619968 | tf_op jit(solution)/shard_map/convert_element_type | solution.py:32
  379.1 1.2 fusion.7
  380.3 1.2 fusion.6
  381.6 1.2 fusion.5
  382.8 1.2 fusion.4
  384.0 1.2 fusion.3
  385.3 1.2 fusion.2
  386.5 1.2 fusion.1
  387.8 1.2 fusion
  389.0 162.5 %all-to-all-done.2 = bf16[16,1024,256]{2,0,1:T(8,128)(2,1)} async-done(((bf16[16,1024,256]{2,0,1:T(8,128)(2,1)}), bf16[16,1024,256]{2,0,1:T(8,128)(2,1)}, u32[]{:S(2)}, u32[]{:S(2)}) %all-to-all-start.2) | async-done | bytes 8388640 | tf_op jit(solution)/shard_map/all_to_all | solution.py:40
  551.6 5.0 all-to-all-start
  556.6 202.2 %all_gather.6 = bf16[2048,16]{0,1:T(8,128)(2,1)S(1)} all-gather(bf16[256,16]{0,1:T(8,128)(2,1)S(1)} %multiply_convert_fusion), channel_id=1, replica_groups=mesh['owner'=4,'rows'=8] {'rows'}, dimensions={0}, use_global_device_ids=true | all-gather | bytes 73728 | tf_op jit(solution)/shard_map/all_gather | solution.py:51
  758.8 6.0 all_gather.7
  764.8 0.8 constant_dynamic-slice_fusion
  765.6 0.7 copy.35
  766.3 0.7 copy.34
  767.6 12.3 %copy.30 = bf16[16,8,256,128]{3,2,1,0:T(8,128)(2,1)} copy(bf16[16,8,256,128]{2,0,3,1:T(8,128)(2,1)} %bitcast.11) | data formatting | bytes 16777216 | tf_op jit(solution)/shard_map/all_to_all | solution.py:38
  779.9 11.4 %copy.33 = bf16[16,128,8,256]{3,2,1,0:T(8,128)(2,1)} copy(bf16[16,128,8,256]{3,0,1,2:T(8,128)(2,1)} %bitcast.14) | data formatting | bytes 16777216 | tf_op jit(solution)/shard_map/all_to_all | solution.py:40
  791.3 13.4 %all_to_all.37 = bf16[16,128,2048]{2,1,0:T(8,128)(2,1)} reshape(bf16[16,128,8,256]{3,2,1,0:T(8,128)(2,1)} %copy.33) | data formatting | bytes 16777216 | tf_op jit(solution)/shard_map/all_to_all | solution.py:40
  804.7 7.9 copy.27
  812.6 0.7 copy.54
  (29 shorter events, 1.0 us)
Async XLA Ops:
  7.2 157.6 %all-reduce.3.cloned.1.call-start = ((), (), s32[]{:S(2)}) async-start(), calls=%async_computation.3 | async-start | bytes 2228224 | tf_op jit(solution)/shard_map/pmax | solution.py:23
  37.3 10.6 %copy-start = (bf16[16,1024,256]{2,1,0:T(8,128)(2,1)S(1)}, bf16[16,1024,256]{2,1,0:T(8,128)(2,1)}, u32[]{:S(2)}) copy-start(bf16[16,1024,256]{2,1,0:T(8,128)(2,1)} %param.13) | copy-start | bytes 25165828
  37.3 40.8 %slice-start = ((s8[16777216]{0:T(1024)(128)(4,1)}), s8[4194304]{0:T(1024)(128)(4,1)S(1)}, s32[]{:S(2)}) async-start(s8[16777216]{0:T(1024)(128)(4,1)} %bitcast.43), calls=%async_computation.4 | async-start | bytes 8388608
  37.3 40.8 %slice-start.1 = ((s8[16777216]{0:T(1024)(128)(4,1)}), s8[4194304]{0:T(1024)(128)(4,1)S(1)}, s32[]{:S(2)}) async-start(s8[16777216]{0:T(1024)(128)(4,1)} %bitcast.43), calls=%async_computation.5 | async-start | bytes 8388608
  37.3 40.8 %slice-start.4 = ((s8[8388608]{0:T(1024)(128)(4,1)}), s8[4194304]{0:T(1024)(128)(4,1)S(1)}, s32[]{:S(2)}) async-start(s8[8388608]{0:T(1024)(128)(4,1)} %bitcast.45), calls=%async_computation.8 | async-start | bytes 8388608
  47.9 30.1 %slice-start.2 = ((s8[16777216]{0:T(1024)(128)(4,1)}), s8[4194304]{0:T(1024)(128)(4,1)S(1)}, s32[]{:S(2)}) async-start(s8[16777216]{0:T(1024)(128)(4,1)} %bitcast.43), calls=%async_computation.6 | async-start | bytes 8388608
  47.9 30.2 %slice-start.3 = ((s8[16777216]{0:T(1024)(128)(4,1)}), s8[4194304]{0:T(1024)(128)(4,1)S(1)}, s32[]{:S(2)}) async-start(s8[16777216]{0:T(1024)(128)(4,1)} %bitcast.43), calls=%async_computation.7 | async-start | bytes 8388608
  47.9 30.2 %slice-start.5 = ((s8[8388608]{0:T(1024)(128)(4,1)}), s8[4194304]{0:T(1024)(128)(4,1)S(1)}, s32[]{:S(2)}) async-start(s8[8388608]{0:T(1024)(128)(4,1)} %bitcast.45), calls=%async_computation.9 | async-start | bytes 8388608
  176.9 5.3 copy-start.1
  176.9 187.8 %all-to-all-start.1 = ((bf16[16,256,1024]{1,0,2:T(8,128)(2,1)}), bf16[16,256,1024]{1,0,2:T(8,128)(2,1)}, u32[]{:S(2)}, u32[]{:S(2)}) async-start(bf16[16,256,1024]{1,0,2:T(8,128)(2,1)} %divide_convert_fusion.1), calls=%async_computation.1 | async-start | bytes 16777216 | tf_op jit(solution)/shard_map/all_to_all | solution.py:38
  205.9 163.7 %copy-start.2 = (f32[16,1024]{1,0:T(8,128)S(1)}, f32[16,1024]{1,0:T(8,128)}, u32[]{:S(2)}) copy-start(f32[16,1024]{1,0:T(8,128)} %get-tuple-element.14) | copy-start | bytes 196612
  364.7 186.9 %all-to-all-start.2 = ((bf16[16,1024,256]{2,0,1:T(8,128)(2,1)}), bf16[16,1024,256]{2,0,1:T(8,128)(2,1)}, u32[]{:S(2)}, u32[]{:S(2)}) async-start(bf16[16,1024,256]{2,0,1:T(8,128)(2,1)} %divide_convert_fusion), calls=%async_computation.2 | async-start | bytes 16777216 | tf_op jit(solution)/shard_map/all_to_all | solution.py:40
  389.0 167.5 %copy-start.3 = (f32[256,16]{0,1:T(8,128)S(1)}, f32[256,16]{0,1:T(8,128)}, u32[]{:S(2)}) copy-start(f32[256,16]{0,1:T(8,128)} %param.14) | copy-start | bytes 49156
  389.0 167.5 %copy-start.4 = (f32[256]{0:T(256)S(1)}, f32[256]{0:T(256)}, u32[]{:S(2)}) copy-start(f32[256]{0:T(256)} %param.15) | copy-start | bytes 3076
  551.6 253.1 %all-to-all-start = ((bf16[8,16,256,128]{3,2,1,0:T(8,128)(2,1)}), bf16[8,16,256,128]{3,2,1,0:T(8,128)(2,1)}, u32[]{:S(2)}, u32[]{:S(2)}) async-start(bf16[8,16,256,128]{3,2,1,0:T(8,128)(2,1)} %fusion), calls=%async_computation | async-start | bytes 16777216 | tf_op jit(solution)/shard_map/all_to_all | solution.py:7
Sparse Core Ops, SparseCore 0:
  82.5 82.2 all-reduce.2
